TPU v7x, 32 devices: a whole 2x2x4 slice. The times are simulated.
32 devices in a mesh: cp: 8 (over z, x), tp: 4 (over y, core).
Axes of the slice: x: 2, y: 2, z: 4, core: 2. Of those that a mesh axis runs over, the one named last changes fastest.
Arguments:
- queries: bfloat16 [1536, 2048], P('cp', 'tp'), may hold values from -128 to 128
- keys: bfloat16 [1536, 256], P('cp'), may hold values from -6 to 6
- values: bfloat16 [1536, 256], P('cp'), may hold values from -6 to 6
- positions: int32 [1536], replicated, may hold values from 0 to 1535, as said below
- out_weight: bfloat16 [2048, 8192], P('tp'), may hold values from -0.125 to 0.125
Outputs:
- mixed: bfloat16 [1536, 8192], P(('cp', 'tp'))
Inputs may be any that keep to these rules, and one draw needn't show every extreme that they name: positions is a permutation of 0 to 1535. The tokens stored at indices d * 192 to (d + 1) * 192 - 1 form two runs of 96 consecutive positions, the first starting at b * 96 and the second at (15 - b) * 96 for some b, each b used by one d.
All inputs are finite; a program needn't handle non-finite values.
Results may differ from a plain program's by a relative error of at most 0.013.
Values may be sent and summed in bfloat16 or wider, within the bound.
A program may use at most 128 MiB of HBM per device.

v0:
```python
import jax
import jax.numpy as jnp
from jax import lax
from jax.sharding import PartitionSpec as P

HEAD = 128
GROUP = 8


def shards(queries, keys, values, positions, out_weight):
    tok_rows = queries.shape[0]
    head_count = queries.shape[1] // HEAD
    score_scale = HEAD ** (-0.5)
    kv_group = lax.axis_index("tp") * head_count // GROUP
    own_keys = lax.dynamic_slice_in_dim(keys, kv_group * HEAD, HEAD, 1)
    own_values = lax.dynamic_slice_in_dim(values, kv_group * HEAD, HEAD, 1)
    query_pos = lax.dynamic_slice_in_dim(positions, lax.axis_index("cp") * tok_rows, tok_rows, 0)
    local_queries = queries.reshape(tok_rows, head_count, HEAD)
    run_max = jnp.full((tok_rows, head_count), -1e30, jnp.float32)
    arrived_keys = lax.all_gather(own_keys, "cp", axis=0, tiled=True)
    arrived_values = lax.all_gather(own_values, "cp", axis=0, tiled=True)
    allowed = (positions[None, :] <= query_pos[:, None])[:, None, :]
    scores = (
        jnp.einsum("qhd,kd->qhk", local_queries, arrived_keys, preferred_element_type=jnp.float32)
        * score_scale
    )
    scores = jnp.where(allowed, scores, -1e30)
    new_max = jnp.maximum(run_max, jnp.max(scores, axis=-1))
    weights = jnp.where(allowed, jnp.exp(scores - new_max[:, :, None]), 0.0)
    run_sum = jnp.sum(weights, axis=-1)
    run_out = jnp.einsum(
        "qhk,kd->qhd",
        weights.astype(jnp.bfloat16),
        arrived_values,
        preferred_element_type=jnp.float32,
    )
    final_state = (new_max, run_sum, run_out)
    run_max, run_sum, run_out = final_state
    attended = (
        (run_out / run_sum[:, :, None]).astype(jnp.bfloat16).reshape(tok_rows, head_count * HEAD)
    )
    return lax.psum_scatter(
        jnp.dot(attended, out_weight, preferred_element_type=jnp.float32).astype(jnp.bfloat16),
        "tp",
        scatter_dimension=0,
        tiled=True,
    )


def solution(mesh):
    in_specs = (P("cp", "tp"), P("cp", None), P("cp", None), P(), P("tp", None))
    out_specs = P(("cp", "tp"), None)
    return jax.shard_map(shards, mesh=mesh, in_specs=in_specs, out_specs=out_specs, check_vma=False)
```

profile of v0, /device:TPU:0, one launch (start us, length us, event | category | flops | bytes accessed | tf_op | source)
XLA Modules:
  0.0 127.3 jit_solution(13655687156293303523)
XLA Ops:
  6.5 0.0 copy-start
  6.5 0.0 copy-start.1
  6.5 0.0 reduce-scatter.2.cloned.1.call-start
  6.5 0.8 constant_dynamic-slice_fusion.1
  7.4 32.8 %all_gather.6 = bf16[1536,128]{1,0:T(8,128)(2,1)S(1)} all-gather(bf16[192,128]{1,0:T(8,128)(2,1)S(1)} %constant_dynamic-slice_fusion.1), channel_id=1, replica_groups=mesh['cp'=8,'tp'=4] {'cp'}, dimensions={0}, use_global_device_ids=true | all-gather | bytes 442368 | tf_op jit(solution)/shard_map/all_gather | solution.py:20
  40.2 0.8 dynamic_slice.9
  40.9 0.9 broadcast_compare_fusion
  41.9 0.0 copy-done
  41.9 1.1 fusion
  43.0 0.0 copy-done.1
  43.0 31.0 %all_gather.7 = bf16[1536,128]{1,0:T(8,128)(2,1)S(1)} all-gather(bf16[192,128]{1,0:T(8,128)(2,1)S(1)} %constant_dynamic-slice_fusion), channel_id=1, replica_groups=mesh['cp'=8,'tp'=4] {'cp'}, dimensions={0}, use_global_device_ids=true | all-gather | bytes 442368 | tf_op jit(solution)/shard_map/all_gather | solution.py:21
  74.0 0.0 slice-start
  74.0 1.5 %fusion.1 = f32[192,4]{0,1:T(4,128)S(1)} fusion(f32[1536,192,4]{0,1,2:T(8,128)S(1)} %get-tuple-element.6, f32[192,4]{0,1:T(4,128)S(1)} %broadcast_maximum_fusion, pred[192,1536]{1,0:T(8,128)(4,1)S(1)} %broadcast_compare_fusion), kind=kLoop, calls=%fused_computation.4 | loop fusion | flops 5897472 | bytes 5019648 | tf_op jit(solution)/shard_map/reduce_sum | solution.py:30
  75.5 0.0 slice-start.1
  75.5 1.4 %fusion.12 = bf16[4,24,8,128]{3,2,1,0:T(8,128)(2,1)S(1)} fusion(f32[1536,192,4]{0,1,2:T(8,128)S(1)} %get-tuple-element.6, f32[192,4]{0,1:T(4,128)S(1)} %broadcast_maximum_fusion, pred[192,1536]{1,0:T(8,128)(4,1)S(1)} %broadcast_compare_fusion, bf16[1536,128]{1,0:T(8,128)(2,1)S(1)} %all_gather.7, f32[192,4]{0,1:T(4,128)S(1)} %fusion.1), kind=kOutput, calls=%fused_computation.10 | convolution fusion | flops 308084736 | bytes 5609472 | tf_op jit(solution)/shard_map/qhk,kd->qhd/dot_general | solution.py:31
  76.9 0.0 slice-done
  76.9 0.9 slice-done.1
  77.8 3.5 %convolution_convert_fusion = bf16[192,8192]{1,0:T(8,128)(2,1)} fusion(bf16[512,8192]{1,0:T(8,128)(2,1)S(1)} %bitcast.41, bf16[4,24,8,128]{3,2,1,0:T(8,128)(2,1)S(1)} %fusion.12), kind=kOutput, calls=%fused_computation | convolution fusion | flops 1612185600 | bytes 11730944 | tf_op jit(solution)/shard_map/dot_general | solution.py:43
  81.3 0.0 reduce-scatter.2.cloned.1.call-update
  81.3 39.2 %reduce-scatter.2.cloned.1.call-done = bf16[48,8192]{1,0:T(8,128)(2,1)} async-done(((bf16[192,8192]{1,0:T(8,128)(2,1)}), bf16[48,8192]{1,0:T(8,128)(2,1)}) %reduce-scatter.2.cloned.1.call-update) | async-done | bytes 786448 | tf_op jit(solution)/shard_map/reduce_scatter | solution.py:42
  (3 shorter events, 0.0 us)
Async XLA Ops:
  6.5 35.3 %copy-start = (bf16[192,512]{1,0:T(8,128)(2,1)S(1)}, bf16[192,512]{1,0:T(8,128)(2,1)}, u32[]{:S(2)}) copy-start(bf16[192,512]{1,0:T(8,128)(2,1)} %param.5) | copy-start | bytes 589828
  6.5 36.4 %copy-start.1 = (bf16[192,256]{1,0:T(8,128)(2,1)S(1)}, bf16[192,256]{1,0:T(8,128)(2,1)}, u32[]{:S(2)}) copy-start(bf16[192,256]{1,0:T(8,128)(2,1)} %param.7) | copy-start | bytes 294916
  6.5 114.0 %reduce-scatter.2.cloned.1.call-start = ((), (), s32[]{:S(2)}) async-start(), calls=%async_computation.1 | async-start | bytes 3932160 | tf_op jit(solution)/shard_map/reduce_scatter | solution.py:42
  74.0 2.9 %slice-start = ((s8[8388608]{0:T(1024)(128)(4,1)}), s8[4194304]{0:T(1024)(128)(4,1)S(1)}, s32[]{:S(2)}) async-start(s8[8388608]{0:T(1024)(128)(4,1)} %bitcast.40), calls=%async_computation.2 | async-start | bytes 8388608
  75.5 2.4 %slice-start.1 = ((s8[8388608]{0:T(1024)(128)(4,1)}), s8[4194304]{0:T(1024)(128)(4,1)S(1)}, s32[]{:S(2)}) async-start(s8[8388608]{0:T(1024)(128)(4,1)} %bitcast.40), calls=%async_computation.3 | async-start | bytes 8388608
Sparse Core Ops, SparseCore 0:
  81.4 39.0 reduce-scatter.1
where the time goes:
time: 128 us; the launch traced here: 127 us
  blocking collectives  63.7 us (50%)
  waiting for transfers between devices  39.2 us (31%)
  between operations  13.4 us (10%)
  matrix products  5.98 us (5%)
  local copies, waits for them, and re-layouts  2.58 us (2%)
  other arithmetic  2.41 us (2%)
    reduce_scatter x1, waiting for transfers between devices, shards(): lax.psum_scatter(jnp.dot(attended, out_weight, preferred_element_type=jnp...  39.2 us
    all_gather x1, blocking collectives, shards(): arrived_keys = lax.all_gather(own_keys, 'cp', axis=0, tiled=True)  32.8 us
    all_gather x1, blocking collectives, shards(): arrived_values = lax.all_gather(own_values, 'cp', axis=0, tiled=True)  31 us
    dot_general x1, matrix products, shards(): jnp.dot(attended, out_weight, preferred_element_type=jnp.float32)  3.47 us
  transfers between devices with their start and end apart: 1, of which 1 were waited for; matrix products, arithmetic and copies ran while one was open for 0% of the time, Pallas kernels for 0%

commit v1 on v0

--- a/solution.py
+++ b/solution.py
@@ -5,6 +5,25 @@
 
 HEAD = 128
 GROUP = 8
+
+
+def joined_along(tiles, dim):
+    lengths = list(tiles.shape[1:])
+    lengths[dim] *= tiles.shape[0]
+    return jnp.moveaxis(tiles, 0, dim).reshape(lengths)
+
+
+def ring_apply(x, axis, dim, work, out_dim):
+    size, here, extent = (lax.axis_size(axis), lax.axis_index(axis), x.shape[dim])
+    right = [(i, (i + 1) % size) for i in range(size)]
+    blocks = []
+    block = x
+    for turn in range(size):
+        coming = block if turn == size - 1 else lax.ppermute(block, axis, right)
+        blocks.append(work(block, (here - turn) % size * extent))
+        block = coming
+    blocks = jnp.stack(blocks)[(here - jnp.arange(size)) % size]
+    return joined_along(blocks, out_dim)
 
 
 def shards(queries, keys, values, positions, out_weight):
@@ -17,11 +36,18 @@
     query_pos = lax.dynamic_slice_in_dim(positions, lax.axis_index("cp") * tok_rows, tok_rows, 0)
     local_queries = queries.reshape(tok_rows, head_count, HEAD)
     run_max = jnp.full((tok_rows, head_count), -1e30, jnp.float32)
-    arrived_keys = lax.all_gather(own_keys, "cp", axis=0, tiled=True)
     arrived_values = lax.all_gather(own_values, "cp", axis=0, tiled=True)
     allowed = (positions[None, :] <= query_pos[:, None])[:, None, :]
     scores = (
-        jnp.einsum("qhd,kd->qhk", local_queries, arrived_keys, preferred_element_type=jnp.float32)
+        ring_apply(
+            own_keys,
+            "cp",
+            0,
+            lambda own_block, offset: jnp.einsum(
+                "qhd,kd->qhk", local_queries, own_block, preferred_element_type=jnp.float32
+            ),
+            2,
+        )
         * score_scale
     )
     scores = jnp.where(allowed, scores, -1e30)

time: 128 us -> 172 us (1.34)
  blocking collectives: 63.7 us -> 31.4 us
  waiting for transfers between devices: 39.2 us -> 69.4 us
  local copies, waits for them, and re-layouts: 2.58 us -> 24.3 us
  matrix products: 5.98 us -> 20.1 us
  other arithmetic: 2.41 us -> 10.3 us
  starting transfers between devices: 0.01 us -> 3.04 us
    ppermute x0 -> x7, waiting for transfers between devices: none -> 34 us  [ring_apply(): coming = block if turn == size - 1 else lax.ppermute(block, axis, right)]
    all_gather x1 -> x0, blocking collectives: 32.8 us -> none  [shards(): arrived_keys = lax.all_gather(own_keys, 'cp', axis=0, tiled=True)]
    mul x0 -> x2, local copies, waits for them, and re-layouts: none -> 14.7 us  [shards(): ring_apply(own_keys, 'cp', 0, lambda own_block, offset: jnp.einsum('qhd,k...]
    dot_general x1 -> x8, matrix products: 1.11 us -> 9.51 us  [shards(): jnp.einsum('qhd,kd->qhk', local_queries, own_block, preferred_element_typ...]
    mul x0 -> x1, other arithmetic: none -> 6.46 us  [shards(): ring_apply(own_keys, 'cp', 0, lambda own_block, offset: jnp.einsum('qhd,k...]
    gather x0 -> x1, local copies, waits for them, and re-layouts: none -> 6.37 us  [ring_apply(): blocks = jnp.stack(blocks)[(here - jnp.arange(size)) % size]]
    reduce_scatter x1, waiting for transfers between devices: 39.2 us -> 35.4 us  [shards(): lax.psum_scatter(jnp.dot(attended, out_weight, preferred_element_type=jnp...]
    dot_general x1, matrix products: 3.47 us -> 6.94 us  [shards(): jnp.dot(attended, out_weight, preferred_element_type=jnp.float32)]
  transfers between devices with their start and end apart: 1 -> 8, of which waited for: 1 -> 7; matrix products, arithmetic and copies ran while one was open for 0% -> 7% of each run, Pallas kernels for 0% -> 0%
where the time goes in v1:
time: 172 us
  waiting for transfers between devices  69.4 us (40%)
  blocking collectives  31.4 us (18%)
  local copies, waits for them, and re-layouts  24.3 us (14%)
  matrix products  20.1 us (12%)
  between operations  13.4 us (8%)
  other arithmetic  10.3 us (6%)
  starting transfers between devices  3.04 us (2%)
    reduce_scatter x1, waiting for transfers between devices, shards(): lax.psum_scatter(jnp.dot(attended, out_weight, preferred_element_type=jnp...  35.4 us
    ppermute x7, waiting for transfers between devices, ring_apply(): coming = block if turn == size - 1 else lax.ppermute(block, axis, right)  34 us
    all_gather x1, blocking collectives, shards(): arrived_values = lax.all_gather(own_values, 'cp', axis=0, tiled=True)  31.4 us
    mul x2, local copies, waits for them, and re-layouts, shards(): ring_apply(own_keys, 'cp', 0, lambda own_block, offset: jnp.einsum('qhd,k...  14.7 us
    dot_general x8, matrix products, shards(): jnp.einsum('qhd,kd->qhk', local_queries, own_block, preferred_element_typ...  9.51 us
    dot_general x1, matrix products, shards(): jnp.dot(attended, out_weight, preferred_element_type=jnp.float32)  6.94 us
    mul x1, other arithmetic, shards(): ring_apply(own_keys, 'cp', 0, lambda own_block, offset: jnp.einsum('qhd,k...  6.46 us
    gather x1, local copies, waits for them, and re-layouts, ring_apply(): blocks = jnp.stack(blocks)[(here - jnp.arange(size)) % size]  6.37 us
  transfers between devices with their start and end apart: 8, of which 7 were waited for; matrix products, arithmetic and copies ran while one was open for 7% of the time, Pallas kernels for 0%

profile of v1, /device:TPU:0, one launch (start us, length us, event | category | flops | bytes accessed | tf_op | source)
XLA Modules:
  0.0 171.9 jit_solution(16083450524662913446)
XLA Ops:
  6.5 0.0 copy-start
  6.5 0.0 reduce-scatter.2.cloned.1.call-start
  6.5 0.8 constant_dynamic-slice_fusion.1
  7.4 3.0 %collective-permute-start = (bf16[192,128]{1,0:T(8,128)(2,1)S(1)}, bf16[192,128]{1,0:T(8,128)(2,1)S(1)}, u32[]{:S(2)}, u32[]{:S(2)}) collective-permute-start(bf16[192,128]{1,0:T(8,128)(2,1)S(1)} %constant_dynamic-slice_fusion.1), channel_id=1, source_target_pairs={{0,4},{4,8},{8,12},{12,16},{16,20},{20,24},{24,28},{28,0},{1,5},{5... | collective-permute-start | bytes 147464 | tf_op jit(solution)/shard_map/ppermute | solution.py:22
  10.3 0.0 copy-done
  10.4 1.2 fusion.9
  11.5 0.8 le.29
  12.3 0.8 dynamic_slice.9
  13.1 0.9 broadcast_compare_fusion.1
  14.0 0.3 broadcast_compare_fusion
  14.3 0.8 constant_dynamic-slice_fusion
  15.1 31.4 %all_gather.3 = bf16[1536,128]{1,0:T(8,128)(2,1)S(1)} all-gather(bf16[192,128]{1,0:T(8,128)(2,1)S(1)} %constant_dynamic-slice_fusion), channel_id=1, replica_groups=mesh['cp'=8,'tp'=4] {'cp'}, dimensions={0}, use_global_device_ids=true | all-gather | bytes 442368 | tf_op jit(solution)/shard_map/all_gather | solution.py:39
  46.5 0.0 collective-permute-done
  46.5 0.1 collective-permute-start.1
  46.6 1.2 fusion.8
  47.7 5.6 %collective-permute-done.1 = bf16[192,128]{1,0:T(8,128)(2,1)S(1)} collective-permute-done((bf16[192,128]{1,0:T(8,128)(2,1)S(1)}, bf16[192,128]{1,0:T(8,128)(2,1)S(1)}, u32[]{:S(2)}, u32[]{:S(2)}) %collective-permute-start.1) | collective-permute-done | bytes 49184 | tf_op jit(solution)/shard_map/ppermute | solution.py:22
  53.3 0.0 collective-permute-start.2
  53.3 1.2 fusion.7
  54.6 5.5 %collective-permute-done.2 = bf16[192,128]{1,0:T(8,128)(2,1)S(1)} collective-permute-done((bf16[192,128]{1,0:T(8,128)(2,1)S(1)}, bf16[192,128]{1,0:T(8,128)(2,1)S(1)}, u32[]{:S(2)}, u32[]{:S(2)}) %collective-permute-start.2) | collective-permute-done | bytes 49184 | tf_op jit(solution)/shard_map/ppermute | solution.py:22
  60.1 0.0 collective-permute-start.3
  60.1 1.3 fusion.6
  61.4 5.5 %collective-permute-done.3 = bf16[192,128]{1,0:T(8,128)(2,1)S(1)} collective-permute-done((bf16[192,128]{1,0:T(8,128)(2,1)S(1)}, bf16[192,128]{1,0:T(8,128)(2,1)S(1)}, u32[]{:S(2)}, u32[]{:S(2)}) %collective-permute-start.3) | collective-permute-done | bytes 49184 | tf_op jit(solution)/shard_map/ppermute | solution.py:22
  66.9 0.0 collective-permute-start.4
  66.9 1.2 fusion.5
  68.1 6.1 %collective-permute-done.4 = bf16[192,128]{1,0:T(8,128)(2,1)S(1)} collective-permute-done((bf16[192,128]{1,0:T(8,128)(2,1)S(1)}, bf16[192,128]{1,0:T(8,128)(2,1)S(1)}, u32[]{:S(2)}, u32[]{:S(2)}) %collective-permute-start.4) | collective-permute-done | bytes 49184 | tf_op jit(solution)/shard_map/ppermute | solution.py:22
  74.2 0.0 collective-permute-start.5
  74.2 1.2 fusion.4
  75.4 5.6 %collective-permute-done.5 = bf16[192,128]{1,0:T(8,128)(2,1)S(1)} collective-permute-done((bf16[192,128]{1,0:T(8,128)(2,1)S(1)}, bf16[192,128]{1,0:T(8,128)(2,1)S(1)}, u32[]{:S(2)}, u32[]{:S(2)}) %collective-permute-start.5) | collective-permute-done | bytes 49184 | tf_op jit(solution)/shard_map/ppermute | solution.py:22
  81.0 0.0 collective-permute-start.6
  81.0 1.2 fusion.3
  82.1 5.6 %collective-permute-done.6 = bf16[192,128]{1,0:T(8,128)(2,1)S(1)} collective-permute-done((bf16[192,128]{1,0:T(8,128)(2,1)S(1)}, bf16[192,128]{1,0:T(8,128)(2,1)S(1)}, u32[]{:S(2)}, u32[]{:S(2)}) %collective-permute-start.6) | collective-permute-done | bytes 49184 | tf_op jit(solution)/shard_map/ppermute | solution.py:22
  87.8 1.2 fusion.2
  88.9 6.4 %gather_fusion = f32[8,192,4,192]{1,3,2,0:T(8,128)} fusion(f32[8,192,4,192]{1,3,2,0:T(8,128)} %fusion.2, s32[1024]{0:T(1024)S(1)} %pad_clamp_fusion), kind=kCustom, calls=%fused_computation | custom fusion | bytes 9437216 | tf_op jit(solution)/shard_map/gather | solution.py:25
  95.3 0.0 copy-start.1
  95.3 6.5 %multiply_bitcast_fusion = f32[192,4,8,192]{0,3,1,2:T(8,128)} fusion(f32[8,192,4,192]{1,3,2,0:T(8,128)} %gather_fusion), kind=kLoop, calls=%fused_computation.3 | loop fusion | flops 1179648 | bytes 9437184 | tf_op jit(solution)/shard_map/mul | solution.py:42
  101.8 0.0 copy-done.1
  101.8 0.9 select_reduce_fusion.1
  102.7 1.7 select_reduce_fusion
  104.4 7.2 %copy.22 = f32[192,4,8,192]{3,2,0,1:T(8,128)} copy(f32[192,4,8,192]{0,3,1,2:T(8,128)} %multiply_bitcast_fusion) | data formatting | bytes 9437184 | tf_op jit(solution)/shard_map/mul | solution.py:42
  111.6 7.5 %mul.31 = f32[192,4,1536]{2,0,1:T(8,128)} reshape(f32[192,4,8,192]{3,2,0,1:T(8,128)} %copy.22) | data formatting | bytes 9437184 | tf_op jit(solution)/shard_map/mul | solution.py:42
  119.1 3.6 %fusion.12 = bf16[4,24,8,128]{3,2,1,0:T(8,128)(2,1)S(1)} fusion(f32[192,4,1536]{2,0,1:T(8,128)} %mul.31, f32[192,4]{0,1:T(4,128)S(1)} %broadcast_maximum_fusion, pred[192,1536]{1,0:T(8,128)(4,1)S(1)} %broadcast_compare_fusion.1, bf16[1536,128]{1,0:T(8,128)(2,1)S(1)} %all_gather.3, f32[192,4]{0,1:T(4,128)S(1)} %select_reduce_fusion), kind=kOutput, calls=%fused_computation.26 | convolution fusion | flops 306905088 | bytes 5609472 | tf_op jit(solution)/shard_map/qhk,kd->qhd/dot_general | solution.py:57
  122.7 6.9 %convolution_convert_fusion = bf16[192,8192]{1,0:T(8,128)(2,1)} fusion(bf16[512,8192]{1,0:T(8,128)(2,1)} %param.9, bf16[4,24,8,128]{3,2,1,0:T(8,128)(2,1)S(1)} %fusion.12), kind=kOutput, calls=%fused_computation.1 | convolution fusion | flops 1612185600 | bytes 11730944 | tf_op jit(solution)/shard_map/dot_general | solution.py:69
  129.6 0.0 reduce-scatter.2.cloned.1.call-update
  129.6 35.4 %reduce-scatter.2.cloned.1.call-done = bf16[48,8192]{1,0:T(8,128)(2,1)} async-done(((bf16[192,8192]{1,0:T(8,128)(2,1)}), bf16[48,8192]{1,0:T(8,128)(2,1)}) %reduce-scatter.2.cloned.1.call-update) | async-done | bytes 786448 | tf_op jit(solution)/shard_map/reduce_scatter | solution.py:68
  (3 shorter events, 0.0 us)
Async XLA Ops:
  6.5 3.8 %copy-start = (bf16[192,512]{1,0:T(8,128)(2,1)S(1)}, bf16[192,512]{1,0:T(8,128)(2,1)}, u32[]{:S(2)}) copy-start(bf16[192,512]{1,0:T(8,128)(2,1)} %param.5) | copy-start | bytes 589828
  6.5 158.5 %reduce-scatter.2.cloned.1.call-start = ((), (), s32[]{:S(2)}) async-start(), calls=%async_computation.1 | async-start | bytes 3932160 | tf_op jit(solution)/shard_map/reduce_scatter | solution.py:68
  7.4 39.1 %collective-permute-start = (bf16[192,128]{1,0:T(8,128)(2,1)S(1)}, bf16[192,128]{1,0:T(8,128)(2,1)S(1)}, u32[]{:S(2)}, u32[]{:S(2)}) collective-permute-start(bf16[192,128]{1,0:T(8,128)(2,1)S(1)} %constant_dynamic-slice_fusion.1), channel_id=1, source_target_pairs={{0,4},{4,8},{8,12},{12,16},{16,20},{20,24},{24,28},{28,0},{1,5},{5... | collective-permute-start | bytes 147464 | tf_op jit(solution)/shard_map/ppermute | solution.py:22
  46.5 6.8 %collective-permute-start.1 = (bf16[192,128]{1,0:T(8,128)(2,1)S(1)}, bf16[192,128]{1,0:T(8,128)(2,1)S(1)}, u32[]{:S(2)}, u32[]{:S(2)}) collective-permute-start(bf16[192,128]{1,0:T(8,128)(2,1)S(1)} %collective-permute-done), channel_id=1, source_target_pairs={{0,4},{4,8},{8,12},{12,16},{16,20},{20,24},{24,28},{28,0},{1,5},{5... | collective-permute-start | bytes 147464 | tf_op jit(solution)/shard_map/ppermute | solution.py:22
  53.3 6.8 %collective-permute-start.2 = (bf16[192,128]{1,0:T(8,128)(2,1)S(1)}, bf16[192,128]{1,0:T(8,128)(2,1)S(1)}, u32[]{:S(2)}, u32[]{:S(2)}) collective-permute-start(bf16[192,128]{1,0:T(8,128)(2,1)S(1)} %collective-permute-done.1), channel_id=1, source_target_pairs={{0,4},{4,8},{8,12},{12,16},{16,20},{20,24},{24,28},{28,0},{1,5},{5... | collective-permute-start | bytes 147464 | tf_op jit(solution)/shard_map/ppermute | solution.py:22
  60.1 6.8 %collective-permute-start.3 = (bf16[192,128]{1,0:T(8,128)(2,1)S(1)}, bf16[192,128]{1,0:T(8,128)(2,1)S(1)}, u32[]{:S(2)}, u32[]{:S(2)}) collective-permute-start(bf16[192,128]{1,0:T(8,128)(2,1)S(1)} %collective-permute-done.2), channel_id=1, source_target_pairs={{0,4},{4,8},{8,12},{12,16},{16,20},{20,24},{24,28},{28,0},{1,5},{5... | collective-permute-start | bytes 147464 | tf_op jit(solution)/shard_map/ppermute | solution.py:22
  66.9 7.3 %collective-permute-start.4 = (bf16[192,128]{1,0:T(8,128)(2,1)S(1)}, bf16[192,128]{1,0:T(8,128)(2,1)S(1)}, u32[]{:S(2)}, u32[]{:S(2)}) collective-permute-start(bf16[192,128]{1,0:T(8,128)(2,1)S(1)} %collective-permute-done.3), channel_id=1, source_target_pairs={{0,4},{4,8},{8,12},{12,16},{16,20},{20,24},{24,28},{28,0},{1,5},{5... | collective-permute-start | bytes 147464 | tf_op jit(solution)/shard_map/ppermute | solution.py:22
  74.2 6.8 %collective-permute-start.5 = (bf16[192,128]{1,0:T(8,128)(2,1)S(1)}, bf16[192,128]{1,0:T(8,128)(2,1)S(1)}, u32[]{:S(2)}, u32[]{:S(2)}) collective-permute-start(bf16[192,128]{1,0:T(8,128)(2,1)S(1)} %collective-permute-done.4), channel_id=1, source_target_pairs={{0,4},{4,8},{8,12},{12,16},{16,20},{20,24},{24,28},{28,0},{1,5},{5... | collective-permute-start | bytes 147464 | tf_op jit(solution)/shard_map/ppermute | solution.py:22
  81.0 6.8 %collective-permute-start.6 = (bf16[192,128]{1,0:T(8,128)(2,1)S(1)}, bf16[192,128]{1,0:T(8,128)(2,1)S(1)}, u32[]{:S(2)}, u32[]{:S(2)}) collective-permute-start(bf16[192,128]{1,0:T(8,128)(2,1)S(1)} %collective-permute-done.5), channel_id=1, source_target_pairs={{0,4},{4,8},{8,12},{12,16},{16,20},{20,24},{24,28},{28,0},{1,5},{5... | collective-permute-start | bytes 147464 | tf_op jit(solution)/shard_map/ppermute | solution.py:22
  95.3 6.5 %copy-start.1 = (f32[8,192,4,192]{1,3,2,0:T(8,128)S(1)}, f32[8,192,4,192]{1,3,2,0:T(8,128)}, u32[]{:S(2)}) copy-start(f32[8,192,4,192]{1,3,2,0:T(8,128)} %gather_fusion) | copy-start | bytes 14155780
Sparse Core Ops, SparseCore 0:
  129.8 35.2 reduce-scatter.1
